TPU v7x, 32 devices: a whole 2x2x4 slice. The times are simulated.
32 devices in a mesh: variant: 4 (over x, core), mesh: 8 (over z, y).
Axes of the slice: x: 2, y: 2, z: 4, core: 2. Of those that a mesh axis runs over, the one named last changes fastest.
Arguments:
- snapshots: float32 [4, 64, 131072], P('variant', None, 'mesh'), may hold values from -12 to 12, as said below
- ref_index: int32 [1], replicated, may hold values from 0 to 3
- weight_codes: int32 [4], replicated, may hold values from 1 to 16
Outputs:
- new_basis: float32 [64, 131072], P(None, 'mesh')
Inputs may be any that keep to these rules, and one draw needn't show every extreme that they name: `snapshots`: each variant's snapshot matrix has full rank 64, and the principal angles between any two variants' spans have tangents below 0.8.
All inputs are finite; a program needn't handle non-finite values.
Results may differ from a plain program's by a relative error of at most 0.0001.
Values sent between devices are 32-bit elements; how exact they have to be, the bound alone decides.
No kernel may reach another device: no remote copies, remote signals or barrier semaphores. Data moves between devices by JAX's collectives and lax.ppermute only.
A program may use at most 64 MiB of HBM per device.

v0:
```python
import math
import jax
import jax.numpy as jnp
from jax import lax
from jax.sharding import PartitionSpec as P

highest = lax.Precision.HIGHEST
atan_coeffs = [(-1.0) ** k / (2 * k + 1) for k in range(24)]
cos_coeffs = [(-1.0) ** k / math.factorial(2 * k) for k in range(24)]
sin_coeffs = [(-1.0) ** k / math.factorial(2 * k + 1) for k in range(24)]


def broadcast(x, axis, root):
    mine = lax.axis_index(axis) == root
    return lax.psum(jnp.where(mine, x, jnp.zeros_like(x)), axis)


def product(left, right):
    return jnp.dot(left, right, precision=highest, preferred_element_type=jnp.float32)


def series(matrix, coeffs):
    eye = jnp.eye(matrix.shape[0], dtype=jnp.float32)
    total = coeffs[-1] * eye
    for coeff in reversed(coeffs[:-1]):
        total = coeff * eye + product(matrix, total)
    return total


def inverse(matrix):
    factor = jnp.linalg.cholesky(product(matrix.T, matrix))
    return jax.scipy.linalg.cho_solve((factor, True), matrix.T)


def on_device(snapshots, ref_index, weight_codes):
    own_snap = snapshots[0]
    root = ref_index[0]
    codes = weight_codes.astype(jnp.float32)
    weight = codes[lax.axis_index("variant")] / jnp.sum(codes)
    eye = jnp.eye(own_snap.shape[0], dtype=jnp.float32)
    scale = jnp.float32(math.sqrt(own_snap.shape[1] * lax.axis_size("mesh")))
    gram_own = lax.psum(product(own_snap, own_snap.T), "mesh")
    lower_own = jnp.linalg.cholesky(gram_own)
    base_own = jax.scipy.linalg.solve_triangular(lower_own, own_snap, lower=True)
    base_ref = broadcast(base_own, "variant", root)
    correlation = lax.psum(product(base_ref, base_own.T), "mesh")
    minv = inverse(correlation)
    tangent = product(minv.T, base_own) - base_ref
    tangent_gram = product(minv.T, minv) - eye
    term = weight * product(series(tangent_gram, atan_coeffs), tangent)
    blended = lax.psum(term, "variant")
    energy = lax.psum(product(blended, blended.T), "mesh")
    mixed = product(series(energy, cos_coeffs), base_ref) + product(
        series(energy, sin_coeffs), blended
    )
    return mixed * scale


def solution(mesh):
    return jax.shard_map(
        on_device,
        mesh=mesh,
        in_specs=(P("variant", None, "mesh"), P(), P()),
        out_specs=P(None, "mesh"),
        check_vma=False,
    )
```

profile of v0, /device:TPU:0, one launch (start us, length us, event | category | flops | bytes accessed | tf_op | source)
XLA Modules:
  0.0 382.1 jit_solution(7541241715108822365)
XLA Ops:
  6.5 6.9 %fusion.3 = f32[64,64]{0,1:T(8,128)S(1)} fusion(f32[1,64,16384]{2,1,0:T(8,128)} %param.4), kind=kOutput, calls=%fused_computation.6 | convolution fusion | flops 805306368 | bytes 4210688 | tf_op jit(solution)/shard_map/dot_general | solution.py:19
  13.5 38.9 %psum.35 = f32[64,64]{0,1:T(8,128)S(1)} all-reduce(f32[64,64]{0,1:T(8,128)S(1)} %fusion.3), channel_id=1, replica_groups=mesh['variant'=4,'mesh'=8] {'mesh'}, use_global_device_ids=true, to_apply=%region_1.0 | all-reduce | flops 4096 | bytes 32768 | tf_op jit(solution)/shard_map/psum | solution.py:42
  52.5 5.8 %cholesky.44 = f32[64,64]{1,0:T(8,128)S(1)} custom-call(f32[64,64]{1,0:T(8,128)S(1)} %fusion.15), custom_call_target="Cholesky" | custom-call | tf_op jit(solution)/shard_map/jit(cholesky)/cholesky | solution.py:43
  58.4 0.6 compare_reduce_fusion.1
  59.0 0.7 fusion.7
  59.7 4.9 %custom-call.13 = f32[1,64,64]{1,2,0:T(8,128)S(1)} custom-call(f32[1,64,64]{2,1,0:T(8,128)S(1)} %fusion.7), custom_call_target="InvertDiagBlocksLowerTriangular" | custom-call | tf_op jit(solution)/shard_map/jit(_solve_triangular)/triangular_solve | solution.py:44
  65.2 9.3 %broadcast_select_fusion = (f32[64,16384]{1,0:T(8,128)}, f32[64,16384]{1,0:T(8,128)}) fusion(pred[]{:T(512)S(6)} %eq.142, f32[1,64,16384]{2,1,0:T(8,128)} %param.4, f32[1,64,64]{1,2,0:T(8,128)S(1)} %custom-call.13), kind=kOutput, calls=%fused_computation.8 | convolution fusion | flops 806354944 | bytes 12599297 | tf_op jit(solution)/shard_map/jit(_solve_triangular)/triangular_solve | solution.py:44
  74.8 0.4 copy-done.1
  75.2 0.6 dynamic_slice.3
  75.7 0.6 convert_reduce_fusion
  77.6 79.8 %all-reduce.3.cloned.1.call-done = f32[64,16384]{1,0:T(8,128)} async-done(((f32[64,16384]{1,0:T(8,128)}), f32[64,16384]{1,0:T(8,128)}) %all-reduce.3.cloned.1.call-update) | async-done | bytes 4194320 | tf_op jit(solution)/shard_map/psum | solution.py:15
  157.4 6.9 %fusion.35 = f32[64,64]{1,0:T(8,128)S(1)} fusion(f32[64,16384]{1,0:T(8,128)} %all-reduce.3.cloned.1.call-done, f32[64,16384]{1,0:T(8,128)} %get-tuple-element.7), kind=kOutput, calls=%fused_computation.114 | convolution fusion | flops 805306368 | bytes 8404992 | tf_op jit(solution)/shard_map/dot_general | solution.py:19
  164.4 37.1 %psum.37 = f32[64,64]{1,0:T(8,128)S(1)} all-reduce(f32[64,64]{1,0:T(8,128)S(1)} %fusion.35), channel_id=1, replica_groups=mesh['variant'=4,'mesh'=8] {'mesh'}, use_global_device_ids=true, to_apply=%region_5.7 | all-reduce | flops 4096 | bytes 32768 | tf_op jit(solution)/shard_map/psum | solution.py:46
  201.8 5.8 %cholesky.55 = f32[64,64]{1,0:T(8,128)S(1)} custom-call(f32[64,64]{1,0:T(8,128)S(1)} %fusion.13), custom_call_target="Cholesky" | custom-call | tf_op jit(solution)/shard_map/jit(cholesky)/cholesky | solution.py:31
  207.7 0.6 compare_reduce_fusion
  208.3 0.7 fusion.8
  209.0 4.9 %custom-call.14 = f32[1,64,64]{1,2,0:T(8,128)S(1)} custom-call(f32[1,64,64]{2,1,0:T(8,128)S(1)} %fusion.8), custom_call_target="InvertDiagBlocksLowerTriangular" | custom-call | tf_op jit(solution)/shard_map/jit(_cho_solve)/triangular_solve | solution.py:32
  218.5 7.2 %convolution_subtract_fusion = f32[64,16384]{1,0:T(8,128)S(1)} fusion(f32[64,16384]{1,0:T(8,128)} %all-reduce.3.cloned.1.call-done, f32[64,64]{1,0:T(8,128)S(1)} %fusion.9, f32[64,16384]{1,0:T(8,128)} %get-tuple-element.7), kind=kOutput, calls=%fused_computation.3 | convolution fusion | flops 806354944 | bytes 12599296 | tf_op jit(solution)/shard_map/dot_general | solution.py:19
  225.7 5.2 %convolution_multiply_fusion = f32[64,16384]{1,0:T(8,128)} fusion(f32[64,64]{1,0:T(8,128)S(1)} %convolution_add_fusion.40, f32[64,16384]{1,0:T(8,128)S(1)} %convolution_subtract_fusion, f32[]{:T(128)S(6)} %div.9), kind=kOutput, calls=%fused_computation.2 | convolution fusion | flops 806354944 | bytes 8404996 | tf_op jit(solution)/shard_map/dot_general | solution.py:19
  230.9 82.1 %all-reduce.5.cloned.1.call-done = f32[64,16384]{1,0:T(8,128)} async-done(((f32[64,16384]{1,0:T(8,128)}), f32[64,16384]{1,0:T(8,128)}) %all-reduce.5.cloned.1.call-update) | async-done | bytes 4194320 | tf_op jit(solution)/shard_map/psum | solution.py:51
  313.0 6.9 %fusion.37 = f32[64,64]{1,0:T(8,128)S(1)} fusion(f32[64,16384]{1,0:T(8,128)} %all-reduce.5.cloned.1.call-done), kind=kOutput, calls=%fused_computation.116 | convolution fusion | flops 805306368 | bytes 4210688 | tf_op jit(solution)/shard_map/dot_general | solution.py:19
  320.0 37.1 %psum.39 = f32[64,64]{1,0:T(8,128)S(1)} all-reduce(f32[64,64]{1,0:T(8,128)S(1)} %fusion.37), channel_id=1, replica_groups=mesh['variant'=4,'mesh'=8] {'mesh'}, use_global_device_ids=true, to_apply=%region_7.9 | all-reduce | flops 4096 | bytes 32768 | tf_op jit(solution)/shard_map/psum | solution.py:52
  364.2 5.6 %fusion.40 = f32[64,16384]{1,0:T(8,128)S(1)} fusion(f32[64,64]{1,0:T(8,128)S(1)} %convolution_add_fusion.20, f32[64,16384]{1,0:T(8,128)} %all-reduce.3.cloned.1.call-done), kind=kOutput, calls=%fused_computation.119 | convolution fusion | flops 805306368 | bytes 8404992 | tf_op jit(solution)/shard_map/dot_general | solution.py:19
  369.9 5.4 %fusion = f32[64,16384]{1,0:T(8,128)} fusion(f32[64,16384]{1,0:T(8,128)S(1)} %fusion.40, f32[64,64]{1,0:T(8,128)S(1)} %convolution_add_fusion.1, f32[64,16384]{1,0:T(8,128)S(1)} %copy-done), kind=kOutput, calls=%fused_computation.1 | convolution fusion | flops 807403520 | bytes 12599296 | tf_op jit(solution)/shard_map/dot_general | solution.py:19
  (83 shorter events, 11.9 us)
Async XLA Ops:
  6.5 150.9 %all-reduce.3.cloned.1.call-start = ((), (), s32[]{:S(2)}) async-start(), calls=%async_computation | async-start | bytes 8388608 | tf_op jit(solution)/shard_map/psum | solution.py:15
  74.5 0.7 copy-start.1
  74.5 238.5 %all-reduce.5.cloned.1.call-start = ((), (), s32[]{:S(2)}) async-start(), calls=%async_computation.1 | async-start | bytes 8388608 | tf_op jit(solution)/shard_map/psum | solution.py:51
  364.2 5.6 %copy-start = (f32[64,16384]{1,0:T(8,128)S(1)}, f32[64,16384]{1,0:T(8,128)}, u32[]{:S(2)}) copy-start(f32[64,16384]{1,0:T(8,128)} %all-reduce.5.cloned.1.call-done) | copy-start | bytes 12582916
Sparse Core Ops, SparseCore 0:
  74.7 82.7 all-reduce.2
  231.0 81.9 all-reduce.4
where the time goes:
time: 382 us
  waiting for transfers between devices  162 us (42%)
  blocking collectives  113 us (30%)
  matrix products  64.9 us (17%)
  other arithmetic  24.8 us (6%)
  between operations  15.9 us (4%)
    psum x1, waiting for transfers between devices, on_device(): blended = lax.psum(term, 'variant')  82.1 us
    psum x1, waiting for transfers between devices, broadcast(): return lax.psum(jnp.where(mine, x, jnp.zeros_like(x)), axis)  79.8 us
    dot_general x74, matrix products, product(): jnp.dot(left, right, precision=highest, preferred_element_type=jnp.float32)  55.2 us
    psum x1, blocking collectives, on_device(): gram_own = lax.psum(product(own_snap, own_snap.T), 'mesh')  38.9 us
    psum x1, blocking collectives, on_device(): energy = lax.psum(product(blended, blended.T), 'mesh')  37.1 us
    psum x1, blocking collectives, on_device(): correlation = lax.psum(product(base_ref, base_own.T), 'mesh')  37.1 us
    another operation x1, matrix products, on_device(): jax.scipy.linalg.solve_triangular(lower_own, own_snap, lower=True)  9.28 us
  transfers between devices with their start and end apart: 2, of which 2 were waited for; matrix products, arithmetic and copies ran while one was open for 0% of the time, Pallas kernels for 0%

commit v1 on v0

--- a/solution.py
+++ b/solution.py
@@ -8,6 +8,14 @@
 atan_coeffs = [(-1.0) ** k / (2 * k + 1) for k in range(24)]
 cos_coeffs = [(-1.0) ** k / math.factorial(2 * k) for k in range(24)]
 sin_coeffs = [(-1.0) ** k / math.factorial(2 * k + 1) for k in range(24)]
+
+
+def add_in_pairs(value, name):
+    peers, total = (lax.axis_size(name), value)
+    for reach in [1 << k for k in range(peers.bit_length() - 1)]:
+        swap = [(i, i ^ reach) for i in range(peers)]
+        total = total + lax.ppermute(total, name, swap)
+    return total
 
 
 def broadcast(x, axis, root):
@@ -48,7 +56,7 @@
     tangent = product(minv.T, base_own) - base_ref
     tangent_gram = product(minv.T, minv) - eye
     term = weight * product(series(tangent_gram, atan_coeffs), tangent)
-    blended = lax.psum(term, "variant")
+    blended = add_in_pairs(term, "variant")
     energy = lax.psum(product(blended, blended.T), "mesh")
     mixed = product(series(energy, cos_coeffs), base_ref) + product(
         series(energy, sin_coeffs), blended

time: 382 us -> 394 us (1.031)
  waiting for transfers between devices: 162 us -> 179 us
  matrix products: 64.9 us -> 60.2 us
  blocking collectives: 113 us -> 109 us
    ppermute x0 -> x2, waiting for transfers between devices: none -> 99.1 us  [add_in_pairs(): total = total + lax.ppermute(total, name, swap)]
    psum x1 -> x0, waiting for transfers between devices: 82.1 us -> none  [on_device(): blended = lax.psum(term, 'variant')]
    dot_general x74, matrix products: 55.2 us -> 50.5 us  [product(): jnp.dot(left, right, precision=highest, preferred_element_type=jnp.float32)]
    psum x1, blocking collectives: 37.1 us -> 33 us  [on_device(): energy = lax.psum(product(blended, blended.T), 'mesh')]
  transfers between devices with their start and end apart: 2 -> 3, of which waited for: 2 -> 3; matrix products, arithmetic and copies ran while one was open for 0% -> 0% of each run, Pallas kernels for 0% -> 0%
where the time goes in v1:
time: 394 us
  waiting for transfers between devices  179 us (45%)
  blocking collectives  109 us (28%)
  matrix products  60.2 us (15%)
  other arithmetic  25.9 us (7%)
  between operations  16 us (4%)
    ppermute x2, waiting for transfers between devices, add_in_pairs(): total = total + lax.ppermute(total, name, swap)  99.1 us
    psum x1, waiting for transfers between devices, broadcast(): return lax.psum(jnp.where(mine, x, jnp.zeros_like(x)), axis)  79.8 us
    dot_general x74, matrix products, product(): jnp.dot(left, right, precision=highest, preferred_element_type=jnp.float32)  50.5 us
    psum x1, blocking collectives, on_device(): gram_own = lax.psum(product(own_snap, own_snap.T), 'mesh')  38.9 us
    psum x1, blocking collectives, on_device(): correlation = lax.psum(product(base_ref, base_own.T), 'mesh')  37.1 us
    psum x1, blocking collectives, on_device(): energy = lax.psum(product(blended, blended.T), 'mesh')  33 us
    another operation x1, matrix products, on_device(): jax.scipy.linalg.solve_triangular(lower_own, own_snap, lower=True)  9.28 us
  transfers between devices with their start and end apart: 3, of which 3 were waited for; matrix products, arithmetic and copies ran while one was open for 0% of the time, Pallas kernels for 0%

profile of v1, /device:TPU:0, one launch (start us, length us, event | category | flops | bytes accessed | tf_op | source)
XLA Modules:
  0.0 394.2 jit_solution(16355510184651458519)
XLA Ops:
  6.5 6.9 %fusion.3 = f32[64,64]{0,1:T(8,128)S(1)} fusion(f32[1,64,16384]{2,1,0:T(8,128)} %param.4), kind=kOutput, calls=%fused_computation.6 | convolution fusion | flops 805306368 | bytes 4210688 | tf_op jit(solution)/shard_map/dot_general | solution.py:27
  13.5 38.9 %psum.28 = f32[64,64]{0,1:T(8,128)S(1)} all-reduce(f32[64,64]{0,1:T(8,128)S(1)} %fusion.3), channel_id=1, replica_groups=mesh['variant'=4,'mesh'=8] {'mesh'}, use_global_device_ids=true, to_apply=%region_1.0 | all-reduce | flops 4096 | bytes 32768 | tf_op jit(solution)/shard_map/psum | solution.py:50
  52.5 5.8 %cholesky.44 = f32[64,64]{1,0:T(8,128)S(1)} custom-call(f32[64,64]{1,0:T(8,128)S(1)} %fusion.15), custom_call_target="Cholesky" | custom-call | tf_op jit(solution)/shard_map/jit(cholesky)/cholesky | solution.py:51
  58.4 0.6 compare_reduce_fusion.1
  59.0 0.7 fusion.7
  59.7 4.9 %custom-call.13 = f32[1,64,64]{1,2,0:T(8,128)S(1)} custom-call(f32[1,64,64]{2,1,0:T(8,128)S(1)} %fusion.7), custom_call_target="InvertDiagBlocksLowerTriangular" | custom-call | tf_op jit(solution)/shard_map/jit(_solve_triangular)/triangular_solve | solution.py:52
  65.3 9.3 %broadcast_select_fusion = (f32[64,16384]{1,0:T(8,128)}, f32[64,16384]{1,0:T(8,128)}) fusion(pred[]{:T(512)S(6)} %eq.142, f32[1,64,16384]{2,1,0:T(8,128)} %param.4, f32[1,64,64]{1,2,0:T(8,128)S(1)} %custom-call.13), kind=kOutput, calls=%fused_computation.8 | convolution fusion | flops 806354944 | bytes 12599297 | tf_op jit(solution)/shard_map/jit(_solve_triangular)/triangular_solve | solution.py:52
  77.6 79.8 %all-reduce.2.cloned.1.call-done = f32[64,16384]{1,0:T(8,128)} async-done(((f32[64,16384]{1,0:T(8,128)}), f32[64,16384]{1,0:T(8,128)}) %all-reduce.2.cloned.1.call-update) | async-done | bytes 4194320 | tf_op jit(solution)/shard_map/psum | solution.py:23
  157.5 6.9 %fusion.35 = f32[64,64]{1,0:T(8,128)S(1)} fusion(f32[64,16384]{1,0:T(8,128)} %all-reduce.2.cloned.1.call-done, f32[64,16384]{1,0:T(8,128)} %get-tuple-element.7), kind=kOutput, calls=%fused_computation.114 | convolution fusion | flops 805306368 | bytes 8404992 | tf_op jit(solution)/shard_map/dot_general | solution.py:27
  164.4 37.1 %psum.30 = f32[64,64]{1,0:T(8,128)S(1)} all-reduce(f32[64,64]{1,0:T(8,128)S(1)} %fusion.35), channel_id=1, replica_groups=mesh['variant'=4,'mesh'=8] {'mesh'}, use_global_device_ids=true, to_apply=%region_5.7 | all-reduce | flops 4096 | bytes 32768 | tf_op jit(solution)/shard_map/psum | solution.py:54
  201.8 5.8 %cholesky.55 = f32[64,64]{1,0:T(8,128)S(1)} custom-call(f32[64,64]{1,0:T(8,128)S(1)} %fusion.13), custom_call_target="Cholesky" | custom-call | tf_op jit(solution)/shard_map/jit(cholesky)/cholesky | solution.py:39
  208.4 0.7 fusion.8
  209.0 4.9 %custom-call.14 = f32[1,64,64]{1,2,0:T(8,128)S(1)} custom-call(f32[1,64,64]{2,1,0:T(8,128)S(1)} %fusion.8), custom_call_target="InvertDiagBlocksLowerTriangular" | custom-call | tf_op jit(solution)/shard_map/jit(_cho_solve)/triangular_solve | solution.py:40
  218.5 7.2 %convolution_subtract_fusion = f32[64,16384]{1,0:T(8,128)S(1)} fusion(f32[64,16384]{1,0:T(8,128)} %all-reduce.2.cloned.1.call-done, f32[64,64]{1,0:T(8,128)S(1)} %fusion.9, f32[64,16384]{1,0:T(8,128)} %get-tuple-element.7), kind=kOutput, calls=%fused_computation.3 | convolution fusion | flops 806354944 | bytes 12599296 | tf_op jit(solution)/shard_map/dot_general | solution.py:27
  225.7 4.0 %convolution_multiply_fusion = f32[64,16384]{1,0:T(8,128)S(1)} fusion(f32[64,64]{1,0:T(8,128)S(1)} %convolution_add_fusion.40, f32[64,16384]{1,0:T(8,128)S(1)} %convolution_subtract_fusion, f32[]{:T(128)S(6)} %div.9), kind=kOutput, calls=%fused_computation.2 | convolution fusion | flops 806354944 | bytes 8404996 | tf_op jit(solution)/shard_map/dot_general | solution.py:27
  229.8 7.1 %collective-permute-done = f32[64,16384]{1,0:T(8,128)S(1)} collective-permute-done((f32[64,16384]{1,0:T(8,128)S(1)}, f32[64,16384]{1,0:T(8,128)S(1)}, u32[]{:S(2)}, u32[]{:S(2)}) %collective-permute-start) | collective-permute-done | bytes 4194336 | tf_op jit(solution)/shard_map/ppermute | solution.py:17
  237.3 0.8 collective-permute-start.1
  238.1 91.9 %collective-permute-done.1 = f32[64,16384]{1,0:T(8,128)S(1)} collective-permute-done((f32[64,16384]{1,0:T(8,128)S(1)}, f32[64,16384]{1,0:T(8,128)S(1)}, u32[]{:S(2)}, u32[]{:S(2)}) %collective-permute-start.1) | collective-permute-done | bytes 4194336 | tf_op jit(solution)/shard_map/ppermute | solution.py:17
  330.0 0.7 add.258
  330.7 2.0 copy-done
  332.7 3.4 fusion.37
  336.1 33.0 %psum.31 = f32[64,64]{1,0:T(8,128)S(1)} all-reduce(f32[64,64]{1,0:T(8,128)S(1)} %fusion.37), channel_id=1, replica_groups=mesh['variant'=4,'mesh'=8] {'mesh'}, use_global_device_ids=true, to_apply=%region_6.8 | all-reduce | flops 4096 | bytes 32768 | tf_op jit(solution)/shard_map/psum | solution.py:60
  376.3 5.6 %fusion.40 = f32[64,16384]{1,0:T(8,128)S(1)} fusion(f32[64,64]{1,0:T(8,128)S(1)} %convolution_add_fusion.20, f32[64,16384]{1,0:T(8,128)} %all-reduce.2.cloned.1.call-done), kind=kOutput, calls=%fused_computation.119 | convolution fusion | flops 805306368 | bytes 8404992 | tf_op jit(solution)/shard_map/dot_general | solution.py:27
  381.9 5.4 %fusion = f32[64,16384]{1,0:T(8,128)} fusion(f32[64,16384]{1,0:T(8,128)S(1)} %fusion.40, f32[64,64]{1,0:T(8,128)S(1)} %convolution_add_fusion.1, f32[64,16384]{1,0:T(8,128)S(1)} %copy-done.1), kind=kOutput, calls=%fused_computation.1 | convolution fusion | flops 807403520 | bytes 12599296 | tf_op jit(solution)/shard_map/dot_general | solution.py:27
  (88 shorter events, 14.6 us)
Async XLA Ops:
  6.5 150.9 %all-reduce.2.cloned.1.call-start = ((), (), s32[]{:S(2)}) async-start(), calls=%async_computation | async-start | bytes 8388608 | tf_op jit(solution)/shard_map/psum | solution.py:23
  74.5 0.7 copy-start.2
  229.7 7.2 %collective-permute-start = (f32[64,16384]{1,0:T(8,128)S(1)}, f32[64,16384]{1,0:T(8,128)S(1)}, u32[]{:S(2)}, u32[]{:S(2)}) collective-permute-start(f32[64,16384]{1,0:T(8,128)S(1)} %convolution_multiply_fusion), channel_id=1, source_target_pairs={{0,8},{8,0},{16,24},{24,16},{1,9},{9,1},{17,25},{25,17},{2,10},{10... | collective-permute-start | bytes 12582920 | tf_op jit(solution)/shard_map/ppermute | solution.py:17
  237.3 92.7 %collective-permute-start.1 = (f32[64,16384]{1,0:T(8,128)S(1)}, f32[64,16384]{1,0:T(8,128)S(1)}, u32[]{:S(2)}, u32[]{:S(2)}) collective-permute-start(f32[64,16384]{1,0:T(8,128)S(1)} %add.257), channel_id=1, source_target_pairs={{0,16},{8,24},{16,0},{24,8},{1,17},{9,25},{17,1},{25,9},{2,18},{10... | collective-permute-start | bytes 12582920 | tf_op jit(solution)/shard_map/ppermute | solution.py:17
  330.7 2.0 copy-start
  376.3 5.6 %copy-start.1 = (f32[64,16384]{1,0:T(8,128)S(1)}, f32[64,16384]{1,0:T(8,128)}, u32[]{:S(2)}) copy-start(f32[64,16384]{1,0:T(8,128)} %copy-done) | copy-start | bytes 12582916
Sparse Core Ops, SparseCore 0:
  74.7 82.7 all-reduce.1
